TPU v7x, 32 devices: a whole 2x2x4 slice. The times are simulated.
32 devices in a mesh: outer: 4 (over y, x), dev: 8 (over z, core).
Axes of the slice: x: 2, y: 2, z: 4, core: 2. Of those that a mesh axis runs over, the one named last changes fastest.
Arguments:
- documents: bfloat16 [6144, 4096], P(('outer', 'dev')), may hold values from -8 to 8
- cluster_of: int32 [6144], replicated, may hold values from 0 to 31, as said below
- neighbours: int32 [32, 4], replicated, may hold values from 0 to 31, as said below
- sharpness: float32 [32], replicated, may hold values from 32 to 64
Outputs:
- density: float32 [6144], P(('outer', 'dev'))
Inputs may be any that keep to these rules, and one draw needn't show every extreme that they name: `cluster_of`: rows b * 192 to (b + 1) * 192 - 1 form block b. Block b names only clusters g * 8 to (g + 1) * 8 - 1, with g = b // 8, and names no cluster more than 48 times; in each group g some cluster is named exactly 48 times by every block of that group; every cluster is named by some row. `neighbours`: row c, with c = g * 8 + h, lists in order the clusters g * 8 + ((h - 1) mod 8), g * 8 + ((h + 1) mod 8), ((g - 1) mod 4) * 8 + ((h + b) mod 8) and ((g + 1) mod 4) * 8 + ((h + d) mod 8), with b and d each in -1, 0, 1.
All inputs are finite; a program needn't handle non-finite values.
Results may differ from a plain program's by a relative error of at most 0.00047.
Values may be sent and summed in bfloat16 or wider, within the bound.
A program may use at most 128 MiB of HBM per device.

v0:
```python
import math

import jax
import jax.numpy as jnp
from jax import lax
from jax.sharding import PartitionSpec as P


def passed_along(block, axis, distance):
    devices = range(lax.axis_size(axis))
    route = [((i - distance) % len(devices), i) for i in devices]
    return lax.ppermute(block, axis, route)


def kernel_block(queries, others, pair_gain):
    products = jnp.einsum("qe,ke->qk", queries, others, preferred_element_type=jnp.float32)
    return jnp.exp(pair_gain * products)


def shards(documents, cluster_of, neighbours, sharpness):
    groups = lax.axis_size("outer")
    owners = lax.axis_size("dev")
    tokens_here = documents.shape[0]
    feature_width = documents.shape[1]
    capacity = max(2, 2 * tokens_here // owners)
    slot_count = owners * capacity
    group_index = lax.axis_index("outer")
    owner_index = lax.axis_index("dev")
    own_cluster = group_index * owners + owner_index
    block_labels = cluster_of.reshape(groups * owners, tokens_here)
    group_of_block = jnp.arange(groups * owners, dtype=jnp.int32) // owners
    local_labels = block_labels - group_of_block[:, None] * owners
    owner_range = jnp.arange(owners, dtype=jnp.int32)
    per_block = jnp.sum(
        (local_labels[:, :, None] == owner_range).astype(jnp.int32), axis=1
    ).reshape(groups, owners, owners)
    cluster_sizes = jnp.sum(per_block, axis=1).reshape(-1)
    own_labels = lax.dynamic_index_in_dim(local_labels, own_cluster, 0, keepdims=False)
    ordinal = jnp.arange(tokens_here, dtype=jnp.int32)
    earlier = ordinal[None, :] < ordinal[:, None]
    repeats = jnp.sum(
        ((own_labels[:, None] == own_labels[None, :]) & earlier).astype(jnp.int32), axis=1
    )
    target = own_labels * capacity + repeats
    placing = (jnp.arange(slot_count, dtype=jnp.int32)[:, None] == target[None, :]).astype(
        jnp.bfloat16
    )
    outgoing = jnp.dot(placing, documents, preferred_element_type=jnp.float32).astype(jnp.bfloat16)
    arrived = lax.all_to_all(
        outgoing.reshape(owners, capacity, feature_width),
        "dev",
        split_axis=0,
        concat_axis=0,
        tiled=True,
    ).reshape(slot_count, feature_width)

    def slot_mask(group_at, owner_at):
        senders = per_block[group_at, :, owner_at]
        return (
            (jnp.arange(capacity, dtype=jnp.int32)[None, :] < senders[:, None])
            .astype(jnp.float32)
            .reshape(-1)
        )

    present = slot_mask(group_index, owner_index)
    centre = jnp.dot(
        present.astype(jnp.bfloat16)[None, :], arrived, preferred_element_type=jnp.float32
    )[0]
    centre = centre / cluster_sizes[own_cluster].astype(jnp.float32)
    centred = arrived.astype(jnp.float32) - centre[None, :]
    scaling = lax.rsqrt(jnp.mean(centred * centred, axis=1) + 1e-06) / math.sqrt(feature_width)
    unit_rows = (centred * (scaling * present)[:, None]).astype(jnp.bfloat16)
    own_gain = sharpness[own_cluster]
    listed = neighbours[own_cluster]
    off_diagonal = 1.0 - jnp.eye(slot_count, dtype=jnp.float32)
    running = jnp.sum(
        kernel_block(unit_rows, unit_rows, own_gain) * (present[None, :] * off_diagonal), axis=1
    )
    beside = [passed_along(unit_rows, "dev", offset) for offset in (1, -1)]
    vertical = []
    for direction, position in ((1, 2), (-1, 3)):
        receiver_group = (group_index + direction) % groups
        wanted = neighbours[receiver_group * owners + owner_index, position]
        delta = (wanted % owners - owner_index + owners) % owners
        picked_rows = jnp.where(
            delta == 1, beside[1], jnp.where(delta == owners - 1, beside[0], unit_rows)
        )
        vertical.append(passed_along(picked_rows, "outer", direction))
    key_sets = [beside[0], beside[1], vertical[0], vertical[1]]
    for position in range(4):
        partner = listed[position]
        partner_group_at = partner // owners
        partner_owner_at = partner % owners
        partner_partner = partner_group_at * owners + partner_owner_at
        pair_gain = 0.5 * (own_gain + sharpness[partner_partner])
        partner = partner_partner
        kernel_terms = kernel_block(unit_rows, key_sets[position], pair_gain)
        key_mask = slot_mask(partner_group_at, partner_owner_at)
        running = running + jnp.sum(kernel_terms * key_mask[None, :], axis=1)
    partner_count = cluster_sizes[own_cluster] - 1 + jnp.sum(cluster_sizes[listed])
    slot_density = jnp.log(running / partner_count.astype(jnp.float32))
    answered = lax.all_to_all(
        slot_density.reshape(owners, capacity), "dev", split_axis=0, concat_axis=0, tiled=True
    ).reshape(-1)
    return answered[target]


def solution(mesh):
    in_specs = (P(("outer", "dev"), None), P(), P(), P())
    out_specs = P(("outer", "dev"))
    return jax.shard_map(shards, mesh=mesh, in_specs=in_specs, out_specs=out_specs, check_vma=False)
```

profile of v0, /device:TPU:0, one launch (start us, length us, event | category | flops | bytes accessed | tf_op | source)
XLA Modules:
  0.0 322.9 jit_solution(3144386299322016211)
XLA Ops:
  0.0 0.9 reshape.344
  1.4 2.7 convolution_convert_fusion
  4.1 6.5 %all-to-all-start = ((bf16[8,48,4096]{2,1,0:T(8,128)(2,1)}), bf16[8,48,4096]{2,1,0:T(8,128)(2,1)}, u32[]{:S(2)}, u32[]{:S(2)}) async-start(bf16[8,48,4096]{2,1,0:T(8,128)(2,1)} %bitcast.58), calls=%async_computation | async-start | bytes 6291456 | tf_op jit(solution)/shard_map/all_to_all | solution.py:49
  23.7 58.5 %all-to-all-done = bf16[8,48,4096]{2,1,0:T(8,128)(2,1)} async-done(((bf16[8,48,4096]{2,1,0:T(8,128)(2,1)}), bf16[8,48,4096]{2,1,0:T(8,128)(2,1)}, u32[]{:S(2)}, u32[]{:S(2)}) %all-to-all-start) | async-done | bytes 3145760 | tf_op jit(solution)/shard_map/all_to_all | solution.py:49
  82.2 2.5 fusion.19
  84.7 2.8 multiply_reduce_fusion
  87.7 4.7 %fusion.1 = bf16[384,4096]{1,0:T(8,128)(2,1)} fusion(bf16[8,48,4096]{2,1,0:T(8,128)(2,1)} %all-to-all-done, f32[384]{0:T(512)S(1)} %reshape.352, f32[4096]{0:T(1024)S(1)} %broadcast_divide_fusion), kind=kLoop, calls=%fused_computation.4 | loop fusion | flops 6291456 | bytes 6309376 | tf_op jit(solution)/shard_map/convert_element_type | solution.py:72
  92.4 1.0 collective-permute-start.1
  107.0 54.8 %collective-permute-done.1 = bf16[384,4096]{1,0:T(8,128)(2,1)} collective-permute-done((bf16[384,4096]{1,0:T(8,128)(2,1)}, bf16[384,4096]{1,0:T(8,128)(2,1)}, u32[]{:S(2)}, u32[]{:S(2)}) %collective-permute-start.1) | collective-permute-done | bytes 3145760 | tf_op jit(solution)/shard_map/ppermute | solution.py:12
  161.8 1.2 collective-permute-done
  162.9 6.1 %select_select_fusion.1 = (bf16[384,4096]{1,0:T(8,128)(2,1)}, bf16[384,4096]{1,0:T(8,128)(2,1)}) fusion(bf16[384,4096]{1,0:T(8,128)(2,1)} %collective-permute-done.1, bf16[384,4096]{1,0:T(8,128)(2,1)} %collective-permute-done, pred[]{:T(512)S(6)} %eq.82, pred[]{:T(512)S(6)} %eq.81, pred[]{:T(512)S(6)} %eq.84, pred[]{:T(512)S(6)} %eq.83, f32[384]{0:T(512)S(1)} %reshape.352, ...), kind=kLoop, calls=%fused_computation.9 | loop fusion | flops 12582912 | bytes 15746564 | tf_op jit(solution)/shard_map/jit(_where)/select_n | solution.py:85
  169.0 1.5 collective-permute-start.2
  170.9 1.6 collective-permute-start.3
  172.5 2.9 multiply_convert_fusion
  175.4 2.5 fusion.12
  177.9 4.7 %fusion.14 = f32[384]{0:T(512)S(1)} fusion(bf16[384,4096]{1,0:T(8,128)(2,1)} %fusion.1, bf16[384,4096]{1,0:T(8,128)(2,1)} %collective-permute-done.1, f32[384]{0:T(512)S(1)} %reshape.354, f32[]{:T(128)S(6)} %mul.182), kind=kOutput, calls=%fused_computation.27 | convolution fusion | flops 1208401536 | bytes 6294532 | tf_op jit(solution)/shard_map/qe,ke->qk/dot_general | solution.py:16
  182.6 4.7 %fusion.13 = f32[384]{0:T(512)S(1)} fusion(bf16[384,4096]{1,0:T(8,128)(2,1)} %fusion.1, bf16[384,4096]{1,0:T(8,128)(2,1)} %collective-permute-done, f32[384]{0:T(512)S(1)} %reshape.353, f32[]{:T(128)S(6)} %mul.173), kind=kOutput, calls=%fused_computation.26 | convolution fusion | flops 1208401536 | bytes 6294532 | tf_op jit(solution)/shard_map/qe,ke->qk/dot_general | solution.py:16
  187.3 54.0 %collective-permute-done.2 = bf16[384,4096]{1,0:T(8,128)(2,1)} collective-permute-done((bf16[384,4096]{1,0:T(8,128)(2,1)}, bf16[384,4096]{1,0:T(8,128)(2,1)}, u32[]{:S(2)}, u32[]{:S(2)}) %collective-permute-start.2) | collective-permute-done | bytes 3145760 | tf_op jit(solution)/shard_map/ppermute | solution.py:12
  241.2 4.7 %fusion.15 = f32[384]{0:T(512)S(1)} fusion(bf16[384,4096]{1,0:T(8,128)(2,1)} %fusion.1, bf16[384,4096]{1,0:T(8,128)(2,1)} %collective-permute-done.2, f32[384]{0:T(512)S(1)} %reshape.355, f32[]{:T(128)S(6)} %mul.188), kind=kOutput, calls=%fused_computation.28 | convolution fusion | flops 1208401536 | bytes 6294532 | tf_op jit(solution)/shard_map/qe,ke->qk/dot_general | solution.py:16
  245.9 60.3 %collective-permute-done.3 = bf16[384,4096]{1,0:T(8,128)(2,1)S(1)} collective-permute-done((bf16[384,4096]{1,0:T(8,128)(2,1)}, bf16[384,4096]{1,0:T(8,128)(2,1)S(1)}, u32[]{:S(2)}, u32[]{:S(2)}) %collective-permute-start.3) | collective-permute-done | bytes 3145760 | tf_op jit(solution)/shard_map/ppermute | solution.py:12
  306.2 3.7 %fusion.16 = f32[384]{0:T(512)S(1)} fusion(bf16[384,4096]{1,0:T(8,128)(2,1)} %fusion.1, bf16[384,4096]{1,0:T(8,128)(2,1)S(1)} %collective-permute-done.3, f32[384]{0:T(512)S(1)} %reshape.356, f32[]{:T(128)S(6)} %mul.195), kind=kOutput, calls=%fused_computation.29 | convolution fusion | flops 1208401536 | bytes 6294532 | tf_op jit(solution)/shard_map/qe,ke->qk/dot_general | solution.py:16
  310.6 3.3 %all-to-all-start.1 = ((f32[8,1,48]{2,1,0:T(1,128)}), f32[8,1,48]{2,1,0:T(1,128)S(1)}, u32[]{:S(2)}, u32[]{:S(2)}) async-start(f32[8,1,48]{2,1,0:T(1,128)} %reshape.359), calls=%async_computation.1 | async-start | bytes 8192 | tf_op jit(solution)/shard_map/all_to_all | solution.py:102
  314.0 5.5 %all-to-all-done.1 = f32[8,1,48]{2,1,0:T(1,128)S(1)} async-done(((f32[8,1,48]{2,1,0:T(1,128)}), f32[8,1,48]{2,1,0:T(1,128)S(1)}, u32[]{:S(2)}, u32[]{:S(2)}) %all-to-all-start.1) | async-done | bytes 1568 | tf_op jit(solution)/shard_map/all_to_all | solution.py:102
  320.7 2.2 gather_fusion.1
  (50 shorter events, 8.6 us)
Async XLA Ops:
  0.0 1.4 copy-start
  4.1 6.5 %copy-start.2 = (s32[32,4]{0,1:T(4,128)S(1)}, s32[32,4]{0,1:T(4,128)}, u32[]{:S(2)}) copy-start(s32[32,4]{0,1:T(4,128)} %param.6) | copy-start | bytes 1540
  4.1 78.1 %all-to-all-start = ((bf16[8,48,4096]{2,1,0:T(8,128)(2,1)}), bf16[8,48,4096]{2,1,0:T(8,128)(2,1)}, u32[]{:S(2)}, u32[]{:S(2)}) async-start(bf16[8,48,4096]{2,1,0:T(8,128)(2,1)} %bitcast.58), calls=%async_computation | async-start | bytes 6291456 | tf_op jit(solution)/shard_map/all_to_all | solution.py:49
  87.7 10.2 %copy-start.1 = (f32[32]{0:T(128)S(1)}, f32[32]{0:T(128)}, u32[]{:S(2)}) copy-start(f32[32]{0:T(128)} %param.7) | copy-start | bytes 388
  92.4 69.4 %collective-permute-start.1 = (bf16[384,4096]{1,0:T(8,128)(2,1)}, bf16[384,4096]{1,0:T(8,128)(2,1)}, u32[]{:S(2)}, u32[]{:S(2)}) collective-permute-start(bf16[384,4096]{1,0:T(8,128)(2,1)} %fusion.1), channel_id=1, source_target_pairs={{1,0},{2,1},{3,2},{4,3},{5,4},{6,5},{7,6},{0,7},{9,8},{10,9},{11,1... | collective-permute-start | bytes 9437192 | tf_op jit(solution)/shard_map/ppermute | solution.py:12
  93.3 69.6 %collective-permute-start = (bf16[384,4096]{1,0:T(8,128)(2,1)}, bf16[384,4096]{1,0:T(8,128)(2,1)}, u32[]{:S(2)}, u32[]{:S(2)}) collective-permute-start(bf16[384,4096]{1,0:T(8,128)(2,1)} %fusion.1), channel_id=1, source_target_pairs={{7,0},{0,1},{1,2},{2,3},{3,4},{4,5},{5,6},{6,7},{15,8},{8,9},{9,10... | collective-permute-start | bytes 9437192 | tf_op jit(solution)/shard_map/ppermute | solution.py:12
  169.0 72.2 %collective-permute-start.2 = (bf16[384,4096]{1,0:T(8,128)(2,1)}, bf16[384,4096]{1,0:T(8,128)(2,1)}, u32[]{:S(2)}, u32[]{:S(2)}) collective-permute-start(bf16[384,4096]{1,0:T(8,128)(2,1)} %get-tuple-element.7), channel_id=1, source_target_pairs={{24,0},{0,8},{8,16},{16,24},{25,1},{1,9},{9,17},{17,25},{26,2},{2,... | collective-permute-start | bytes 9437192 | tf_op jit(solution)/shard_map/ppermute | solution.py:12
  170.9 135.3 %collective-permute-start.3 = (bf16[384,4096]{1,0:T(8,128)(2,1)}, bf16[384,4096]{1,0:T(8,128)(2,1)S(1)}, u32[]{:S(2)}, u32[]{:S(2)}) collective-permute-start(bf16[384,4096]{1,0:T(8,128)(2,1)} %get-tuple-element.8), channel_id=1, source_target_pairs={{8,0},{16,8},{24,16},{0,24},{9,1},{17,9},{25,17},{1,25},{10,2},{18... | collective-permute-start | bytes 9437192 | tf_op jit(solution)/shard_map/ppermute | solution.py:12
  310.6 8.9 %all-to-all-start.1 = ((f32[8,1,48]{2,1,0:T(1,128)}), f32[8,1,48]{2,1,0:T(1,128)S(1)}, u32[]{:S(2)}, u32[]{:S(2)}) async-start(f32[8,1,48]{2,1,0:T(1,128)} %reshape.359), calls=%async_computation.1 | async-start | bytes 8192 | tf_op jit(solution)/shard_map/all_to_all | solution.py:102
where the time goes:
time: 324 us; the launch traced here: 323 us
  waiting for transfers between devices  234 us (72%)
  matrix products  25.4 us (8%)
  between operations  21.2 us (7%)
  other arithmetic  19.2 us (6%)
  starting transfers between devices  13.9 us (4%)
  local copies, waits for them, and re-layouts  8.99 us (3%)
    ppermute x4, waiting for transfers between devices, passed_along(): return lax.ppermute(block, axis, route)  170 us
    all_to_all x1, waiting for transfers between devices, shards(): lax.all_to_all(outgoing.reshape(owners, capacity, feature_width), 'dev',...  58.5 us
    dot_general x5, matrix products, kernel_block(): jnp.einsum('qe,ke->qk', queries, others, preferred_element_type=jnp.float32)  20.2 us
    convert_element_type x2, other arithmetic, shards(): unit_rows = (centred * (scaling * present)[:, None]).astype(jnp.bfloat16)  7.56 us
    all_to_all x1, starting transfers between devices, shards(): lax.all_to_all(outgoing.reshape(owners, capacity, feature_width), 'dev',...  6.49 us
  transfers between devices with their start and end apart: 6, of which 6 were waited for; matrix products, arithmetic and copies ran while one was open for 8% of the time, Pallas kernels for 0%

commit v1 on v0

--- a/solution.py
+++ b/solution.py
@@ -105,7 +105,77 @@
     return answered[target]
 
 
+def lookup(table, index):
+    hit = index[:, None] == jnp.arange(table.shape[0], dtype=jnp.int32)[None, :]
+    return jnp.sum(jnp.where(hit, table[None, :], jnp.zeros((), table.dtype)), axis=1)
+
+
+def gathered(documents, cluster_of, neighbours, sharpness):
+    groups = lax.axis_size("outer")
+    owners = lax.axis_size("dev")
+    tokens_here, feature_width = documents.shape
+    group_index = lax.axis_index("outer")
+    owner_index = lax.axis_index("dev")
+    clusters = groups * owners
+    group_rows = owners * tokens_here
+    cluster_range = jnp.arange(clusters, dtype=jnp.int32)
+    sizes = jnp.sum((cluster_of[:, None] == cluster_range[None, :]).astype(jnp.int32), axis=0)
+
+    def labels_at(group_at):
+        start = (group_at * owners + owner_index) * tokens_here
+        return lax.dynamic_slice_in_dim(cluster_of, start, tokens_here)
+
+    previous = (group_index + groups - 1) % groups
+    following = (group_index + 1) % groups
+    own = labels_at(group_index)
+    local = own - group_index * owners
+    local_range = jnp.arange(owners, dtype=jnp.int32)
+    member = (local_range[:, None] == local[None, :]).astype(jnp.bfloat16)
+    sums = lax.psum(jnp.dot(member, documents, preferred_element_type=jnp.float32), "dev")
+    own_sizes = lax.dynamic_slice_in_dim(sizes, group_index * owners, owners)
+    means = sums / own_sizes.astype(jnp.float32)[:, None]
+    centre = jnp.dot(
+        member.astype(jnp.float32).T,
+        means,
+        precision=lax.Precision.HIGHEST,
+        preferred_element_type=jnp.float32,
+    )
+    centred = documents.astype(jnp.float32) - centre
+    scaling = lax.rsqrt(jnp.mean(centred * centred, axis=1) + 1e-06) / math.sqrt(feature_width)
+    unit_rows = (centred * scaling[:, None]).astype(jnp.bfloat16)
+    from_previous = passed_along(unit_rows, "outer", 1)
+    from_following = passed_along(unit_rows, "outer", -1)
+    keys = lax.all_gather(unit_rows, "dev", axis=0, tiled=True)
+    key_labels = lax.dynamic_slice_in_dim(cluster_of, group_index * group_rows, group_rows)
+    key_gain = lookup(sharpness, key_labels)
+
+    def partial(queries, labels, positions, own_too):
+        products = jnp.einsum("qe,ke->qk", queries, keys, preferred_element_type=jnp.float32)
+        gain = 0.5 * (lookup(sharpness, labels)[:, None] + key_gain[None, :])
+        wanted = jnp.zeros(products.shape, jnp.bool_)
+        for position in positions:
+            listed = lookup(neighbours[:, position], labels)
+            wanted = wanted | (listed[:, None] == key_labels[None, :])
+        if own_too:
+            at = owner_index * tokens_here + jnp.arange(tokens_here, dtype=jnp.int32)
+            other = at[:, None] != jnp.arange(group_rows, dtype=jnp.int32)[None, :]
+            wanted = wanted | ((labels[:, None] == key_labels[None, :]) & other)
+        return jnp.sum(jnp.where(wanted, jnp.exp(gain * products), 0.0), axis=1)
+
+    back_previous = partial(from_previous, labels_at(previous), (3,), False)
+    back_following = partial(from_following, labels_at(following), (2,), False)
+    running = partial(unit_rows, own, (0, 1), True)
+    running = running + passed_along(back_previous, "outer", -1)
+    running = running + passed_along(back_following, "outer", 1)
+    counts = sizes - 1
+    for position in range(neighbours.shape[1]):
+        counts = counts + lookup(sizes, neighbours[:, position])
+    return jnp.log(running / lookup(counts, own).astype(jnp.float32))
+
+
 def solution(mesh):
+    small = mesh.shape["dev"] <= 8
     in_specs = (P(("outer", "dev"), None), P(), P(), P())
     out_specs = P(("outer", "dev"))
-    return jax.shard_map(shards, mesh=mesh, in_specs=in_specs, out_specs=out_specs, check_vma=False)
+    body = gathered if small else shards
+    return jax.shard_map(body, mesh=mesh, in_specs=in_specs, out_specs=out_specs, check_vma=False)

time: 324 us -> 227 us (0.70)
  waiting for transfers between devices: 234 us -> 169 us
  other arithmetic: 19.2 us -> 4.04 us
  starting transfers between devices: 13.9 us -> 5.69 us
  matrix products: 25.4 us -> 33.2 us
  between operations: 21.2 us -> 13.5 us
  local copies, waits for them, and re-layouts: 8.99 us -> 1.47 us
    ppermute x4, waiting for transfers between devices: 170 us -> 34 us  [passed_along(): return lax.ppermute(block, axis, route)]
    all_gather x0 -> x1, waiting for transfers between devices: none -> 77.3 us  [gathered(): keys = lax.all_gather(unit_rows, 'dev', axis=0, tiled=True)]
    all_to_all x2 -> x0, waiting for transfers between devices: 64 us -> none  [the longest x1 58.5 us: shards(): lax.all_to_all(outgoing.reshape(owners, capacity, feature_width), 'dev',...]
    psum x0 -> x1, waiting for transfers between devices: none -> 57.5 us  [gathered(): lax.psum(jnp.dot(member, documents, preferred_element_type=jnp.float32),...]
    all_to_all x2 -> x0, starting transfers between devices: 9.82 us -> none  [the longest x1 6.49 us: shards(): lax.all_to_all(outgoing.reshape(owners, capacity, feature_width), 'dev',...]
    dot_general x7 -> x5, matrix products: 25.4 us -> 33.2 us  [the longest x3 28 us: partial(): jnp.einsum('qe,ke->qk', queries, keys, preferred_element_type=jnp.float32)]
    convert_element_type x7 -> x2, other arithmetic: 7.92 us -> 1.62 us  [the longest x1 1.54 us: gathered(): unit_rows = (centred * scaling[:, None]).astype(jnp.bfloat16)]
    select_n x3 -> x0, other arithmetic: 6.1 us -> none  [the longest x1 6.09 us: shards(): jnp.where(delta == 1, beside[1], jnp.where(delta == owners - 1, beside[0]...]
  transfers between devices with their start and end apart: 6 -> 6, of which waited for: 6 -> 3; matrix products, arithmetic and copies ran while one was open for 8% -> 13% of each run, Pallas kernels for 0% -> 0%
where the time goes in v1:
time: 227 us
  waiting for transfers between devices  169 us (74%)
  matrix products  33.2 us (15%)
  between operations  13.5 us (6%)
  starting transfers between devices  5.69 us (3%)
  other arithmetic  4.04 us (2%)
    all_gather x1, waiting for transfers between devices, gathered(): keys = lax.all_gather(unit_rows, 'dev', axis=0, tiled=True)  77.3 us
    psum x1, waiting for transfers between devices, gathered(): lax.psum(jnp.dot(member, documents, preferred_element_type=jnp.float32),...  57.5 us
    ppermute x4, waiting for transfers between devices, passed_along(): return lax.ppermute(block, axis, route)  34 us
    dot_general x3, matrix products, partial(): jnp.einsum('qe,ke->qk', queries, keys, preferred_element_type=jnp.float32)  28 us
    ppermute x4, starting transfers between devices, passed_along(): return lax.ppermute(block, axis, route)  5.65 us
  transfers between devices with their start and end apart: 6, of which 3 were waited for; matrix products, arithmetic and copies ran while one was open for 13% of the time, Pallas kernels for 0%

profile of v1, /device:TPU:0, one launch (start us, length us, event | category | flops | bytes accessed | tf_op | source)
XLA Modules:
  0.0 226.7 jit_solution(15810836763792392852)
XLA Ops:
  6.5 0.9 broadcast_subtract_fusion
  7.5 2.4 %fusion.13 = f32[8,4096]{1,0:T(8,128)} fusion(bf16[192,4096]{1,0:T(8,128)(2,1)} %param.4, s32[192]{0:T(256)S(1)} %get-tuple-element.15), kind=kOutput, calls=%fused_computation.44 | convolution fusion | flops 12584448 | bytes 1704704 | tf_op jit(solution)/shard_map/dot_general | solution.py:134
  9.9 0.2 convert_reduce_fusion
  10.1 0.1 dynamic-slice_convert_fusion
  10.2 57.5 %all-reduce.2.cloned.1.call-done = f32[8,4096]{1,0:T(8,128)} async-done(((f32[8,4096]{1,0:T(8,128)}), f32[8,4096]{1,0:T(8,128)}) %all-reduce.2.cloned.1.call-update) | async-done | bytes 131088 | tf_op jit(solution)/shard_map/psum | solution.py:134
  67.7 2.8 %multiply_reduce_fusion = (f32[192]{0:T(256)S(1)}, f32[192,4096]{1,0:T(8,128)S(1)}) fusion(f32[8,4096]{1,0:T(8,128)} %all-reduce.2.cloned.1.call-done, f32[8]{0:T(128)S(1)} %dynamic-slice_convert_fusion, s32[192]{0:T(256)S(1)} %get-tuple-element.15, bf16[192,4096]{1,0:T(8,128)(2,1)S(1)} %copy-done.1), kind=kOutput, calls=%fused_computation.2 | convolution fusion | flops 78677312 | bytes 4851232 | tf_op jit(solution)/shard_map/dot_general | solution.py:137
  70.5 1.5 multiply_convert_fusion
  72.1 1.4 copy-done
  73.4 2.4 %collective-permute-start.2 = (bf16[192,4096]{1,0:T(8,128)(2,1)S(1)}, bf16[192,4096]{1,0:T(8,128)(2,1)S(1)}, u32[]{:S(2)}, u32[]{:S(2)}) collective-permute-start(bf16[192,4096]{1,0:T(8,128)(2,1)S(1)} %copy-done), channel_id=1, source_target_pairs={{8,0},{16,8},{24,16},{0,24},{9,1},{17,9},{25,17},{1,25},{10,2},{18... | collective-permute-start | bytes 4718600 | tf_op jit(solution)/shard_map/ppermute | solution.py:12
  75.8 0.1 dynamic_slice.16
  75.9 0.1 select_reduce_fusion.3
  76.0 0.1 select_reduce_fusion.5
  76.1 0.1 select_reduce_fusion.4
  76.3 0.2 select_reduce_fusion.12
  76.5 0.1 select_reduce_fusion.8
  76.6 0.1 select_reduce_fusion
  76.7 34.0 %collective-permute-done.2 = bf16[192,4096]{1,0:T(8,128)(2,1)S(1)} collective-permute-done((bf16[192,4096]{1,0:T(8,128)(2,1)S(1)}, bf16[192,4096]{1,0:T(8,128)(2,1)S(1)}, u32[]{:S(2)}, u32[]{:S(2)}) %collective-permute-start.2) | collective-permute-done | bytes 1572896 | tf_op jit(solution)/shard_map/ppermute | solution.py:12
  110.7 77.3 %all-gather.2.cloned.1.call-done = bf16[1536,4096]{1,0:T(8,128)(2,1)} async-done(((bf16[192,4096]{1,0:T(8,128)(2,1)}), bf16[1536,4096]{1,0:T(8,128)(2,1)}) %all-gather.2.cloned.1.call-update) | async-done | bytes 12582928 | tf_op jit(solution)/shard_map/all_gather | solution.py:148
  188.0 9.1 %fusion.8 = f32[192]{0:T(256)S(1)} fusion(bf16[192,4096]{1,0:T(8,128)(2,1)S(1)} %collective-permute-done.2, bf16[1536,4096]{1,0:T(8,128)(2,1)} %all-gather.2.cloned.1.call-done, f32[192]{0:T(256)S(1)} %get-tuple-element.9, f32[1536]{0:T(1024)S(1)} %select_reduce_fusion, s32[1536]{0:T(1024)S(1)} %dynamic_slice.16, s32[192]{0:T(256)S(1)} %select_reduce_fusion.3), kind=kOutput, calls=%fused_computation.14 | convolution fusion | flops 2417688320 | bytes 14170368 | tf_op jit(solution)/shard_map/qe,ke->qk/dot_general | solution.py:153
  197.1 1.5 collective-permute-start.3
  198.6 9.6 %fusion.7 = f32[192]{0:T(256)S(1)} fusion(bf16[192,4096]{1,0:T(8,128)(2,1)} %collective-permute-done, bf16[1536,4096]{1,0:T(8,128)(2,1)} %all-gather.2.cloned.1.call-done, f32[192]{0:T(256)S(1)} %get-tuple-element.8, f32[1536]{0:T(1024)S(1)} %select_reduce_fusion, s32[1536]{0:T(1024)S(1)} %dynamic_slice.16, s32[192]{0:T(256)S(1)} %select_reduce_fusion.5), kind=kOutput, calls=%fused_computation.13 | convolution fusion | flops 2417688320 | bytes 14170368 | tf_op jit(solution)/shard_map/qe,ke->qk/dot_general | solution.py:153
  208.2 1.7 collective-permute-start.1
  209.9 9.4 %fusion.6 = f32[192]{0:T(256)S(1)} fusion(bf16[192,4096]{1,0:T(8,128)(2,1)S(1)} %copy-done, bf16[1536,4096]{1,0:T(8,128)(2,1)} %all-gather.2.cloned.1.call-done, f32[1536]{0:T(1024)S(1)} %select_reduce_fusion, f32[192]{0:T(256)S(1)} %get-tuple-element.10, s32[192]{0:T(256)S(1)} %iota_add_fusion, s32[1536]{0:T(1024)S(1)} %dynamic_slice.16, ...), kind=kOutput, calls=%fused_computation.12 | convolution fusion | flops 2419457792 | bytes 14172672 | tf_op jit(solution)/shard_map/qe,ke->qk/dot_general | solution.py:153
  219.3 0.6 fusion.16
  (21 shorter events, 0.2 us)
Async XLA Ops:
  6.5 3.4 %copy-start.2 = (s32[6144]{0:T(1024)S(1)}, s32[6144]{0:T(1024)}, u32[]{:S(2)}) copy-start(s32[6144]{0:T(1024)} %param.5) | copy-start | bytes 73732
  6.5 61.2 %copy-start.1 = (bf16[192,4096]{1,0:T(8,128)(2,1)S(1)}, bf16[192,4096]{1,0:T(8,128)(2,1)}, u32[]{:S(2)}) copy-start(bf16[192,4096]{1,0:T(8,128)(2,1)} %param.4) | copy-start | bytes 4718596
  6.5 61.2 %all-reduce.2.cloned.1.call-start = ((), (), s32[]{:S(2)}) async-start(), calls=%async_computation | async-start | bytes 262144 | tf_op jit(solution)/shard_map/psum | solution.py:134
  9.9 178.2 %all-gather.2.cloned.1.call-start = ((), (), s32[]{:S(2)}) async-start(), calls=%async_computation.1 | async-start | bytes 14155776 | tf_op jit(solution)/shard_map/all_gather | solution.py:148
  72.0 1.4 copy-start
  72.0 3.9 %copy-start.3 = (s32[32,4]{0,1:T(4,128)S(1)}, s32[32,4]{0,1:T(4,128)}, u32[]{:S(2)}) copy-start(s32[32,4]{0,1:T(4,128)} %param.6) | copy-start | bytes 1540
  72.0 4.0 %copy-start.4 = (f32[32]{0:T(128)S(1)}, f32[32]{0:T(128)}, u32[]{:S(2)}) copy-start(f32[32]{0:T(128)} %param.7) | copy-start | bytes 388
  73.4 37.3 %collective-permute-start.2 = (bf16[192,4096]{1,0:T(8,128)(2,1)S(1)}, bf16[192,4096]{1,0:T(8,128)(2,1)S(1)}, u32[]{:S(2)}, u32[]{:S(2)}) collective-permute-start(bf16[192,4096]{1,0:T(8,128)(2,1)S(1)} %copy-done), channel_id=1, source_target_pairs={{8,0},{16,8},{24,16},{0,24},{9,1},{17,9},{25,17},{1,25},{10,2},{18... | collective-permute-start | bytes 4718600 | tf_op jit(solution)/shard_map/ppermute | solution.py:12
  76.2 122.4 %collective-permute-start = (bf16[192,4096]{1,0:T(8,128)(2,1)S(1)}, bf16[192,4096]{1,0:T(8,128)(2,1)}, u32[]{:S(2)}, u32[]{:S(2)}) collective-permute-start(bf16[192,4096]{1,0:T(8,128)(2,1)S(1)} %copy-done), channel_id=1, source_target_pairs={{24,0},{0,8},{8,16},{16,24},{25,1},{1,9},{9,17},{17,25},{26,2},{2,... | collective-permute-start | bytes 4718600 | tf_op jit(solution)/shard_map/ppermute | solution.py:12
  197.1 22.2 %collective-permute-start.3 = (f32[192]{0:T(256)S(1)}, f32[192]{0:T(256)S(1)}, u32[]{:S(2)}, u32[]{:S(2)}) collective-permute-start(f32[192]{0:T(256)S(1)} %fusion.8), channel_id=1, source_target_pairs={{24,0},{0,8},{8,16},{16,24},{25,1},{1,9},{9,17},{17,25},{26,2},{2,... | collective-permute-start | bytes 2312 | tf_op jit(solution)/shard_map/ppermute | solution.py:12
  208.2 11.1 %collective-permute-start.1 = (f32[192]{0:T(256)S(1)}, f32[192]{0:T(256)S(1)}, u32[]{:S(2)}, u32[]{:S(2)}) collective-permute-start(f32[192]{0:T(256)S(1)} %fusion.7), channel_id=1, source_target_pairs={{8,0},{16,8},{24,16},{0,24},{9,1},{17,9},{25,17},{1,25},{10,2},{18... | collective-permute-start | bytes 2312 | tf_op jit(solution)/shard_map/ppermute | solution.py:12
Sparse Core Ops, SparseCore 0:
  10.0 57.6 all-reduce.1
  72.2 115.8 all-gather.1

commit v2 on v1

--- a/solution.py
+++ b/solution.py
@@ -1,8 +1,11 @@
+import functools
 import math
 
 import jax
 import jax.numpy as jnp
 from jax import lax
+from jax.experimental import pallas as pl
+from jax.experimental.pallas import tpu as pltpu
 from jax.sharding import PartitionSpec as P
 
 
@@ -105,6 +108,366 @@
     return answered[target]
 
 
+MESH = pl.DeviceIdType.MESH
+
+
+def meet(peers, expected):
+    barrier = pltpu.get_barrier_semaphore()
+    for present, peer in peers:
+        if present is None:
+            pl.semaphore_signal(barrier, inc=1, device_id=peer, device_id_type=MESH)
+        else:
+
+            @pl.when(present)
+            def _(peer=peer):
+                pl.semaphore_signal(barrier, inc=1, device_id=peer, device_id_type=MESH)
+
+    pl.semaphore_wait(barrier, expected)
+
+
+def sum_kernel(owners, part_ref, out_ref, landed, reduced, gathered_sums, sems):
+    me = lax.axis_index("dev")
+    width = part_ref.shape[1] // owners
+
+    def span(at):
+        return pl.ds(pl.multiple_of(at * width, 128), width)
+
+    others = [lax.rem(me + step, owners) for step in range(1, owners)]
+    meet([(None, {"dev": peer}) for peer in others], owners - 1)
+
+    def scatter(step):
+        return pltpu.make_async_remote_copy(
+            src_ref=part_ref.at[:, span(others[step])],
+            dst_ref=landed.at[step],
+            send_sem=sems.at[0, step],
+            recv_sem=sems.at[1, step],
+            device_id={"dev": others[step]},
+            device_id_type=MESH,
+        )
+
+    def spread(step):
+        return pltpu.make_async_remote_copy(
+            src_ref=reduced,
+            dst_ref=gathered_sums.at[step],
+            send_sem=sems.at[2, step],
+            recv_sem=sems.at[3, step],
+            device_id={"dev": others[step]},
+            device_id_type=MESH,
+        )
+
+    for step in range(owners - 1):
+        scatter(step).start()
+    total = part_ref[:, span(me)]
+    for step in range(owners - 1):
+        scatter(step).wait_recv()
+        total = total + landed[step]
+    reduced[...] = total
+    for step in range(owners - 1):
+        spread(step).start()
+    out_ref[:, span(me)] = total
+    for step in range(owners - 1):
+        spread(step).wait_recv()
+        sender = lax.rem(me + owners - 1 - step, owners)
+        out_ref[:, span(sender)] = gathered_sums[step]
+    for step in range(owners - 1):
+        scatter(step).wait_send()
+        spread(step).wait_send()
+
+
+def summed(part):
+    owners = lax.axis_size("dev")
+    rows, width = part.shape
+    block = (owners - 1, rows, width // owners)
+    return pl.pallas_call(
+        functools.partial(sum_kernel, owners),
+        out_shape=jax.ShapeDtypeStruct(part.shape, jnp.float32),
+        in_specs=[pl.BlockSpec(memory_space=pltpu.VMEM)],
+        out_specs=pl.BlockSpec(memory_space=pltpu.VMEM),
+        scratch_shapes=[
+            pltpu.VMEM(block, jnp.float32),
+            pltpu.VMEM(block[1:], jnp.float32),
+            pltpu.VMEM(block, jnp.float32),
+            pltpu.SemaphoreType.DMA((4, owners - 1)),
+        ],
+        compiler_params=pltpu.CompilerParams(collective_id=0, has_side_effects=True),
+        name="mean_sums",
+    )(part)
+
+
+def return_kernel(owners, cols_ref, rows_ref, out_ref, landed, sems):
+    me = lax.axis_index("dev")
+    group = lax.axis_index("outer")
+    beside = group + 1 - 2 * lax.rem(group, 2)
+    opposite = 3 - group
+    others = [lax.rem(me + step, owners) for step in range(1, owners)]
+    peers = [{"dev": peer} for peer in others] + [{"outer": beside}, {"outer": opposite}]
+    sources = [cols_ref.at[peer] for peer in others] + [rows_ref.at[1], rows_ref.at[2]]
+    meet([(None, peer) for peer in peers], len(peers))
+    copies = [
+        pltpu.make_async_remote_copy(
+            src_ref=sources[k],
+            dst_ref=landed.at[k],
+            send_sem=sems.at[0, k],
+            recv_sem=sems.at[1, k],
+            device_id=peers[k],
+            device_id_type=MESH,
+        )
+        for k in range(len(peers))
+    ]
+    for copy in copies:
+        copy.start()
+    total = rows_ref[0]
+    for k, copy in enumerate(copies):
+        copy.wait_recv()
+        total = total + landed[k]
+    out_ref[...] = total
+    for copy in copies:
+        copy.wait_send()
+
+
+def returned(cols, rows):
+    owners = lax.axis_size("dev")
+    peers = owners + 1
+    return pl.pallas_call(
+        functools.partial(return_kernel, owners),
+        out_shape=jax.ShapeDtypeStruct(cols.shape[1:], jnp.float32),
+        in_specs=[pl.BlockSpec(memory_space=pltpu.VMEM)] * 2,
+        out_specs=pl.BlockSpec(memory_space=pltpu.VMEM),
+        scratch_shapes=[
+            pltpu.VMEM((peers,) + cols.shape[1:], jnp.float32),
+            pltpu.SemaphoreType.DMA((2, peers)),
+        ],
+        compiler_params=pltpu.CompilerParams(collective_id=2, has_side_effects=True),
+        name="return_sums",
+    )(cols, rows)
+
+
+PIECES = 4
+
+
+def pair_kernel(
+    unit_ref, lists_ref, gain_ref, klist_ref, kgain_ref,
+    acc_ref, cols_ref, queries, keys, z_sems, core_sems, key_sems, side_sems,
+):
+    dev = lax.axis_index("dev")
+    group = lax.axis_index("outer")
+    z, core = dev // 2, lax.rem(dev, 2)
+    rows = unit_ref.shape[0]
+    piece = rows // PIECES
+    partner = {"dev": 2 * z + 1 - core}
+    above = {"dev": lax.rem(dev + 2, 8)}
+    below = {"dev": lax.rem(dev + 6, 8)}
+    beside = {"outer": group + 1 - 2 * lax.rem(group, 2)}
+    across = {"outer": lax.rem(group + 2, 4)}
+    meet(
+        [(None, partner), (None, beside), (None, across), (z < 3, above), (z > 0, below)],
+        3 + jnp.where(z < 3, 1, 0) + jnp.where(z > 0, 1, 0),
+    )
+
+    def part(k):
+        return pl.ds(pl.multiple_of(k * piece, piece), piece)
+
+    def remote(src, dst, send_sem, recv_sem, device):
+        return pltpu.make_async_remote_copy(
+            src_ref=src, dst_ref=dst, send_sem=send_sem, recv_sem=recv_sem,
+            device_id=device, device_id_type=MESH,
+        )
+
+    def hop(unit, k, device, own=False):
+        at = 2 * unit + core
+        src = unit_ref.at[part(k)] if own else keys.at[at, part(k)]
+        return remote(src, keys.at[at, part(k)], z_sems.at[unit, k], key_sems.at[at, k], device)
+
+    def share(unit, k, own=False):
+        at = 2 * unit + core
+        src = unit_ref.at[part(k)] if own else keys.at[at, part(k)]
+        return remote(
+            src, keys.at[at, part(k)], core_sems.at[unit, k], key_sems.at[at, k], partner
+        )
+
+    def side(k):
+        return remote(
+            unit_ref.at[part(k)], queries.at[1, part(k)],
+            side_sems.at[0, k], side_sems.at[1, k], beside,
+        )
+
+    def relay(k):
+        return remote(
+            queries.at[1, part(k)], queries.at[2, part(k)],
+            side_sems.at[2, k], side_sems.at[3, k], across,
+        )
+
+    def arrived(at, k):
+        remote(
+            keys.at[at, part(k)], keys.at[at, part(k)],
+            core_sems.at[0, k], key_sems.at[at, k], partner,
+        ).wait_recv()
+
+    def own_sends(k, act):
+        act(side(k))
+
+        @pl.when(z < 2)
+        def _():
+            act(hop(z, k, above, own=True))
+
+        @pl.when(z == 3)
+        def _():
+            act(hop(z, k, below, own=True))
+
+        act(share(z, k, own=True))
+
+    def start(copy):
+        copy.start()
+
+    def sent(copy):
+        copy.wait_send()
+
+    def loop(body):
+        lax.fori_loop(0, PIECES, lambda k, carry: (body(k), carry)[1], 0)
+
+    loop(lambda k: own_sends(k, start))
+    queries[0] = unit_ref[...]
+    keys[dev] = unit_ref[...]
+    acc_ref[...] = jnp.zeros_like(acc_ref)
+    cols_ref[...] = jnp.zeros_like(cols_ref)
+
+    def first(k):
+        side(k).wait_recv()
+        relay(k).start()
+
+        @pl.when((z == 1) | (z == 2))
+        def _():
+            unit = z - 1
+            arrived(2 * unit + core, k)
+            hop(unit, k, above).start()
+            share(unit, k).start()
+
+        @pl.when(z == 2)
+        def _():
+            arrived(6 + core, k)
+            share(3, k).start()
+
+    loop(first)
+
+    def late(k):
+        @pl.when(z == 3)
+        def _():
+            arrived(2 + core, k)
+            share(1, k).start()
+
+        relay(k).wait_recv()
+
+    loop(late)
+
+    def stage(k):
+        @pl.when(z >= 2)
+        def _():
+            arrived(core, k)
+            share(0, k).start()
+
+        @pl.when(z == 2)
+        def _():
+            hop(0, k, above).start()
+
+        unit = jnp.where(
+            k == 0, z, jnp.where(k == 1, jnp.where(z == 1, 0, 1), jnp.where(k == 2, 3, 0))
+        )
+        ready = (
+            (k == 0)
+            | ((k == 1) & (z > 0))
+            | ((k == 2) & (z == 2))
+            | ((k == 3) & (z >= 2))
+        )
+
+        @pl.when(ready)
+        def _():
+            loop(lambda p: arrived(2 * unit + 1 - core, p))
+            foreign = jnp.where(k > 0, 1.0, 0.0)
+
+            def one(c, carry):
+                at = 2 * unit + c
+                products = lax.dot_general(
+                    queries[...].reshape(3 * rows, unit_ref.shape[1]),
+                    keys[at],
+                    (((1,), (1,)), ((), ())),
+                    preferred_element_type=jnp.float32,
+                )
+                down = jnp.zeros((1, rows), jnp.float32)
+                kl = klist_ref[at, 0]
+                for b in range(3):
+                    terms = jnp.exp(
+                        0.5 * (gain_ref[b] + kgain_ref[at]) * products[b * rows : (b + 1) * rows]
+                    )
+                    wanted = lists_ref[b, 1] == kl
+                    if b == 0:
+                        wanted = wanted | (lists_ref[0, 2] == kl) | (lists_ref[0, 3] == kl)
+                        shape = (rows, rows)
+                        same = lax.broadcasted_iota(jnp.int32, shape, 0) == (
+                            lax.broadcasted_iota(jnp.int32, shape, 1)
+                        )
+                        wanted = wanted & jnp.logical_not(same & (at == dev))
+                        back = wanted
+                    else:
+                        back = lists_ref[b, 0] == klist_ref[at, b]
+                    acc_ref[b] += jnp.where(wanted, terms, 0.0)
+                    down = down + jnp.sum(jnp.where(back, terms, 0.0), axis=0, keepdims=True)
+                cols_ref[at] = down * foreign
+                return carry
+
+            lax.fori_loop(0, 2, one, 0)
+
+    loop(stage)
+
+    def finish(k):
+        own_sends(k, sent)
+        sent(relay(k))
+
+        @pl.when((z == 1) | (z == 2))
+        def _():
+            sent(hop(z - 1, k, above))
+            sent(share(z - 1, k))
+
+        @pl.when(z == 2)
+        def _():
+            sent(share(3, k))
+            sent(hop(0, k, above))
+
+        @pl.when(z == 3)
+        def _():
+            sent(share(1, k))
+
+        @pl.when(z >= 2)
+        def _():
+            sent(share(0, k))
+
+    loop(finish)
+
+
+def paired(unit_rows, lists, gain, klists, kgain):
+    rows, width = unit_rows.shape
+    return pl.pallas_call(
+        pair_kernel,
+        out_shape=[
+            jax.ShapeDtypeStruct((3, rows, rows), jnp.float32),
+            jax.ShapeDtypeStruct((8, 1, rows), jnp.float32),
+        ],
+        in_specs=[pl.BlockSpec(memory_space=pltpu.VMEM)] * 5,
+        out_specs=[pl.BlockSpec(memory_space=pltpu.VMEM)] * 2,
+        scratch_shapes=[
+            pltpu.VMEM((3, rows, width), jnp.bfloat16),
+            pltpu.VMEM((8, rows, width), jnp.bfloat16),
+            pltpu.SemaphoreType.DMA((4, PIECES)),
+            pltpu.SemaphoreType.DMA((4, PIECES)),
+            pltpu.SemaphoreType.DMA((8, PIECES)),
+            pltpu.SemaphoreType.DMA((4, PIECES)),
+        ],
+        compiler_params=pltpu.CompilerParams(
+            collective_id=1, has_side_effects=True, vmem_limit_bytes=56 * 1024 * 1024
+        ),
+        name="pairs",
+    )(unit_rows, lists, gain, klists, kgain)
+
+
 def lookup(table, index):
     hit = index[:, None] == jnp.arange(table.shape[0], dtype=jnp.int32)[None, :]
     return jnp.sum(jnp.where(hit, table[None, :], jnp.zeros((), table.dtype)), axis=1)
@@ -125,13 +488,11 @@
         start = (group_at * owners + owner_index) * tokens_here
         return lax.dynamic_slice_in_dim(cluster_of, start, tokens_here)
 
-    previous = (group_index + groups - 1) % groups
-    following = (group_index + 1) % groups
     own = labels_at(group_index)
     local = own - group_index * owners
     local_range = jnp.arange(owners, dtype=jnp.int32)
     member = (local_range[:, None] == local[None, :]).astype(jnp.bfloat16)
-    sums = lax.psum(jnp.dot(member, documents, preferred_element_type=jnp.float32), "dev")
+    sums = summed(jnp.dot(member, documents, preferred_element_type=jnp.float32))
     own_sizes = lax.dynamic_slice_in_dim(sizes, group_index * owners, owners)
     means = sums / own_sizes.astype(jnp.float32)[:, None]
     centre = jnp.dot(
@@ -143,30 +504,34 @@
     centred = documents.astype(jnp.float32) - centre
     scaling = lax.rsqrt(jnp.mean(centred * centred, axis=1) + 1e-06) / math.sqrt(feature_width)
     unit_rows = (centred * scaling[:, None]).astype(jnp.bfloat16)
-    from_previous = passed_along(unit_rows, "outer", 1)
-    from_following = passed_along(unit_rows, "outer", -1)
-    keys = lax.all_gather(unit_rows, "dev", axis=0, tiled=True)
+
+    even = group_index % 2 == 0
+    beside = labels_at(group_index + 1 - 2 * (group_index % 2))
+    across = labels_at(3 - group_index)
+    before = neighbours[:, 2]
+    after = neighbours[:, 3]
+    seen_beside = jnp.where(even, before, after)
+    seen_across = jnp.where(even, after, before)
+    listed = [
+        [own, own, lookup(neighbours[:, 0], own), lookup(neighbours[:, 1], own)],
+        [beside] + [lookup(seen_beside, beside)] * 3,
+        [across] + [lookup(seen_across, across)] * 3,
+    ]
+    lists = jnp.stack([jnp.stack(block) for block in listed])[..., None]
+    gain = jnp.stack([lookup(sharpness, block[0]) for block in listed])[..., None]
     key_labels = lax.dynamic_slice_in_dim(cluster_of, group_index * group_rows, group_rows)
-    key_gain = lookup(sharpness, key_labels)
-
-    def partial(queries, labels, positions, own_too):
-        products = jnp.einsum("qe,ke->qk", queries, keys, preferred_element_type=jnp.float32)
-        gain = 0.5 * (lookup(sharpness, labels)[:, None] + key_gain[None, :])
-        wanted = jnp.zeros(products.shape, jnp.bool_)
-        for position in positions:
-            listed = lookup(neighbours[:, position], labels)
-            wanted = wanted | (listed[:, None] == key_labels[None, :])
-        if own_too:
-            at = owner_index * tokens_here + jnp.arange(tokens_here, dtype=jnp.int32)
-            other = at[:, None] != jnp.arange(group_rows, dtype=jnp.int32)[None, :]
-            wanted = wanted | ((labels[:, None] == key_labels[None, :]) & other)
-        return jnp.sum(jnp.where(wanted, jnp.exp(gain * products), 0.0), axis=1)
-
-    back_previous = partial(from_previous, labels_at(previous), (3,), False)
-    back_following = partial(from_following, labels_at(following), (2,), False)
-    running = partial(unit_rows, own, (0, 1), True)
-    running = running + passed_along(back_previous, "outer", -1)
-    running = running + passed_along(back_following, "outer", 1)
+    key_shape = (owners, 1, 1, tokens_here)
+    klists = jnp.concatenate(
+        [
+            key_labels.reshape(key_shape),
+            lookup(seen_across, key_labels).reshape(key_shape),
+            lookup(seen_beside, key_labels).reshape(key_shape),
+        ],
+        axis=1,
+    )
+    kgain = lookup(sharpness, key_labels).reshape(owners, 1, tokens_here)
+    acc, cols = paired(unit_rows, lists, gain, klists, kgain)
+    running = returned(cols, jnp.sum(acc, axis=2)[:, None, :])[0]
     counts = sizes - 1
     for position in range(neighbours.shape[1]):
         counts = counts + lookup(sizes, neighbours[:, position])
@@ -174,7 +539,7 @@
 
 
 def solution(mesh):
-    small = mesh.shape["dev"] <= 8
+    small = mesh.shape["dev"] == 8 and mesh.shape["outer"] == 4
     in_specs = (P(("outer", "dev"), None), P(), P(), P())
     out_specs = P(("outer", "dev"))
     body = gathered if small else shards

time: 227 us -> 128 us (0.56)
  waiting for transfers between devices: 169 us -> 0 us
  Pallas kernels: 0 us -> 111 us
  matrix products: 33.2 us -> 5.09 us
  between operations: 13.5 us -> 0.12 us
  starting transfers between devices: 5.69 us -> 0 us
  other arithmetic: 4.04 us -> 7.33 us
  local copies, waits for them, and re-layouts: 1.47 us -> 4.67 us
    pallas_call x0 -> x3, Pallas kernels: none -> 111 us  [the longest x1 53.7 us: paired(): pl.pallas_call(pair_kernel, out_shape=[jax.ShapeDtypeStruct((3, rows, row...]
    all_gather x1 -> x0, waiting for transfers between devices: 77.3 us -> none  [gathered(): keys = lax.all_gather(unit_rows, 'dev', axis=0, tiled=True)]
    psum x1 -> x0, waiting for transfers between devices: 57.5 us -> none  [gathered(): lax.psum(jnp.dot(member, documents, preferred_element_type=jnp.float32),...]
    ppermute x4 -> x0, waiting for transfers between devices: 34 us -> none  [passed_along(): return lax.ppermute(block, axis, route)]
    dot_general x3 -> x0, matrix products: 28 us -> none  [partial(): jnp.einsum('qe,ke->qk', queries, keys, preferred_element_type=jnp.float32)]
    ppermute x4 -> x0, starting transfers between devices: 5.65 us -> none  [passed_along(): return lax.ppermute(block, axis, route)]
    broadcast_in_dim x1 -> x3, local copies, waits for them, and re-layouts: 0.01 us -> 2.96 us  [the longest x1 1.46 us: gathered(): lists = jnp.stack([jnp.stack(block) for block in listed])[..., None]]
  transfers between devices with their start and end apart: 6 -> 0, of which waited for: 3 -> 0; matrix products, arithmetic and copies ran while one was open for 13% -> 0% of each run, Pallas kernels for 0% -> 0%
where the time goes in v2:
time: 128 us
  Pallas kernels  111 us (87%)
  other arithmetic  7.33 us (6%)
  matrix products  5.09 us (4%)
  local copies, waits for them, and re-layouts  4.67 us (4%)
    pallas_call x1, Pallas kernels, paired(): pl.pallas_call(pair_kernel, out_shape=[jax.ShapeDtypeStruct((3, rows, row...  53.7 us
    pallas_call x1, Pallas kernels, returned(): pl.pallas_call(functools.partial(return_kernel, owners), out_shape=jax.Sh...  41.3 us
    pallas_call x1, Pallas kernels, summed(): pl.pallas_call(functools.partial(sum_kernel, owners), out_shape=jax.Shape...  15.6 us
    dot_general x1, matrix products, gathered(): jnp.dot(member.astype(jnp.float32).T, means, precision=lax.Precision.HIGH...  2.73 us

profile of v2, /device:TPU:0, one launch (start us, length us, event | category | flops | bytes accessed | tf_op | source)
XLA Modules:
  0.0 127.8 jit_solution(13147753356137115006)
XLA Ops:
  0.0 0.9 broadcast_subtract_fusion
  0.9 2.4 %fusion.2.part_ref = f32[8,4096]{1,0:T(8,128)} fusion(bf16[192,4096]{1,0:T(8,128)(2,1)} %param.4, s32[192]{0:T(256)S(1)} %get-tuple-element.21), kind=kOutput, calls=%fused_computation.33 | convolution fusion | flops 12584448 | bytes 1704704 | tf_op jit(solution)/shard_map/dot_general | solution.py:495
  3.3 15.6 %mean_sums.1 = f32[8,4096]{1,0:T(8,128)} custom-call(f32[8,4096]{1,0:T(8,128)} %fusion.2.part_ref), custom_call_target="tpu_custom_call" | custom-call | tf_op jit(solution)/shard_map/mean_sums/pallas_call | solution.py:181
  18.9 0.9 convert_reduce_fusion
  19.9 2.7 %multiply_reduce_fusion = (f32[192]{0:T(256)S(1)}, f32[192,4096]{1,0:T(8,128)S(1)}) fusion(f32[8,4096]{1,0:T(8,128)} %mean_sums.1, f32[8]{0:T(128)S(1)} %dynamic-slice_convert_fusion, s32[192]{0:T(256)S(1)} %get-tuple-element.21, bf16[192,4096]{1,0:T(8,128)(2,1)S(1)} %copy-done), kind=kOutput, calls=%fused_computation.2 | convolution fusion | flops 78677312 | bytes 4851232 | tf_op jit(solution)/shard_map/dot_general | solution.py:498
  22.6 1.5 %multiply_convert_fusion.unit_ref = bf16[192,4096]{1,0:T(8,128)(2,1)} fusion(f32[192,4096]{1,0:T(8,128)S(1)} %get-tuple-element.32, f32[192]{0:T(256)S(1)} %rsqrt_multiply_fusion), kind=kLoop, calls=%fused_computation.1 | loop fusion | flops 1572864 | bytes 4719360 | tf_op jit(solution)/shard_map/convert_element_type | solution.py:506
  24.1 0.2 select_reduce_fusion.14
  24.4 0.1 select_reduce_fusion.3
  24.5 0.1 select_reduce_fusion.8
  24.6 1.5 %copy.7.lists_ref = s32[3,4,192,1]{3,2,1,0:T(8,128)} copy(s32[3,4,192,1]{2,1,0,3:T(4,128)S(1)} %add_bitcast_fusion) | data formatting | bytes 18432 | tf_op jit(solution)/shard_map/broadcast_in_dim | solution.py:520
  26.1 0.1 select_reduce_fusion.6
  26.2 0.9 copy.8.gain_ref
  27.1 0.8 dynamic_slice.19
  27.9 0.1 select_reduce_fusion.2
  28.0 0.1 reshape.63
  28.1 0.1 reshape.64
  28.3 0.6 pad_add_fusion.klist_ref
  28.9 0.1 select_reduce_fusion
  29.0 0.7 reshape.65.kgain_ref
  29.7 53.7 %pairs.1 = (f32[3,192,192]{2,1,0:T(8,128)}, f32[8,1,192]{2,1,0:T(1,128)}) custom-call(bf16[192,4096]{1,0:T(8,128)(2,1)} %multiply_convert_fusion.unit_ref, s32[3,4,192,1]{3,2,1,0:T(8,128)} %copy.7.lists_ref, f32[3,192,1]{2,1,0:T(8,128)} %copy.8.gain_ref, s32[8,3,1,192]{3,2,1,0:T(1,128)} %pad_add_fusion.klist_ref, f32[8,1,192]{2,1,0:T(1,128)} %reshape.65.kgain_ref), custom_call_target="tpu_custom_call" | custom-call | tf_op jit(solution)/shard_map/pairs/pallas_call | solution.py:448
  83.3 1.2 reduce_sum.174
  84.6 0.6 broadcast_in_dim.184.rows_ref
  85.2 41.3 %return_sums.1 = f32[1,192]{1,0:T(1,128)} custom-call(f32[8,1,192]{2,1,0:T(1,128)} %get-tuple-element.7.cols_ref, f32[3,1,192]{2,1,0:T(1,128)} %broadcast_in_dim.184.rows_ref), custom_call_target="tpu_custom_call" | custom-call | tf_op jit(solution)/shard_map/return_sums/pallas_call | solution.py:231
  126.5 1.2 fusion.5
  (17 shorter events, 0.3 us)
Async XLA Ops:
  0.0 19.9 %copy-start = (bf16[192,4096]{1,0:T(8,128)(2,1)S(1)}, bf16[192,4096]{1,0:T(8,128)(2,1)}, u32[]{:S(2)}) copy-start(bf16[192,4096]{1,0:T(8,128)(2,1)} %param.4) | copy-start | bytes 4718596
  22.6 1.5 %copy-start.1 = (s32[32,4]{0,1:T(4,128)S(1)}, s32[32,4]{0,1:T(4,128)}, u32[]{:S(2)}) copy-start(s32[32,4]{0,1:T(4,128)} %param.6) | copy-start | bytes 1540
  22.6 3.5 %copy-start.2 = (f32[32]{0:T(128)S(1)}, f32[32]{0:T(128)}, u32[]{:S(2)}) copy-start(f32[32]{0:T(128)} %param.7) | copy-start | bytes 388

commit v3 on v2

--- a/solution.py
+++ b/solution.py
@@ -242,12 +242,13 @@
     )(cols, rows)
 
 
-PIECES = 4
+PIECES = 6
 
 
 def pair_kernel(
-    unit_ref, lists_ref, gain_ref, klist_ref, kgain_ref,
-    acc_ref, cols_ref, queries, keys, z_sems, core_sems, key_sems, side_sems,
+    unit_ref, labels_ref, neighbours_ref, sharpness_ref, rows_ref, cols_ref,
+    lists_ref, gain_ref, klist_ref, kgain_ref, acc_ref,
+    queries, keys, z_sems, core_sems, key_sems, side_sems,
 ):
     dev = lax.axis_index("dev")
     group = lax.axis_index("outer")
@@ -326,6 +327,43 @@
         lax.fori_loop(0, PIECES, lambda k, carry: (body(k), carry)[1], 0)
 
     loop(lambda k: own_sends(k, start))
+    square = (rows, rows)
+    same = lax.broadcasted_iota(jnp.int32, square, 0) == lax.broadcasted_iota(jnp.int32, square, 1)
+
+    def chosen(read, labels, base, zero):
+        found = jnp.full(labels.shape, zero, jnp.float32)
+        for h in range(8):
+            found = jnp.where(labels == base + h, read(base + h), found)
+        return found
+
+    def listed(position):
+        return lambda c: neighbours_ref[c, position].astype(jnp.float32)
+
+    def sharp(c):
+        return sharpness_ref[c]
+
+    def upright(row):
+        return jnp.sum(jnp.where(same, row, 0.0), axis=1, keepdims=True)
+
+    odd = lax.rem(group, 2)
+    toward = {0: None, 1: 2 + odd, 2: 3 - odd}
+    for b, at_group in enumerate((group, group + 1 - 2 * odd, 3 - group)):
+        base = at_group * 8
+        labels = labels_ref[base + dev]
+        lists_ref[b, 0] = upright(labels.astype(jnp.float32))
+        gain_ref[b] = upright(chosen(sharp, labels, base, 0.0))
+        positions = (0, 1) if b == 0 else (toward[b],)
+        for slot, position in enumerate(positions):
+            lists_ref[b, 1 + slot] = upright(chosen(listed(position), labels, base, 0.0))
+
+    def key_tables(at):
+        labels = labels_ref[group * 8 + at]
+        klist_ref[at, 0] = labels.astype(jnp.float32)
+        kgain_ref[at] = chosen(sharp, labels, group * 8, 0.0)
+        klist_ref[at, 1] = chosen(listed(3 - odd), labels, group * 8, 0.0)
+        klist_ref[at, 2] = chosen(listed(2 + odd), labels, group * 8, 0.0)
+
+    lax.fori_loop(0, 8, lambda at, carry: (key_tables(at), carry)[1], 0)
     queries[0] = unit_ref[...]
     keys[dev] = unit_ref[...]
     acc_ref[...] = jnp.zeros_like(acc_ref)
@@ -376,7 +414,7 @@
             (k == 0)
             | ((k == 1) & (z > 0))
             | ((k == 2) & (z == 2))
-            | ((k == 3) & (z >= 2))
+            | ((k == PIECES - 1) & (z >= 2))
         )
 
         @pl.when(ready)
@@ -400,11 +438,7 @@
                     )
                     wanted = lists_ref[b, 1] == kl
                     if b == 0:
-                        wanted = wanted | (lists_ref[0, 2] == kl) | (lists_ref[0, 3] == kl)
-                        shape = (rows, rows)
-                        same = lax.broadcasted_iota(jnp.int32, shape, 0) == (
-                            lax.broadcasted_iota(jnp.int32, shape, 1)
-                        )
+                        wanted = wanted | (lists_ref[0, 2] == kl) | (lists_ref[0, 0] == kl)
                         wanted = wanted & jnp.logical_not(same & (at == dev))
                         back = wanted
                     else:
@@ -417,6 +451,9 @@
             lax.fori_loop(0, 2, one, 0)
 
     loop(stage)
+    for b in range(3):
+        across_lanes = jnp.sum(acc_ref[b], axis=1, keepdims=True)
+        rows_ref[b] = jnp.sum(jnp.where(same, across_lanes, 0.0), axis=0, keepdims=True)
 
     def finish(k):
         own_sends(k, sent)
@@ -443,17 +480,24 @@
     loop(finish)
 
 
-def paired(unit_rows, lists, gain, klists, kgain):
+def paired(unit_rows, labels, neighbours, sharpness):
     rows, width = unit_rows.shape
+    vmem = pl.BlockSpec(memory_space=pltpu.VMEM)
+    smem = pl.BlockSpec(memory_space=pltpu.SMEM)
     return pl.pallas_call(
         pair_kernel,
         out_shape=[
-            jax.ShapeDtypeStruct((3, rows, rows), jnp.float32),
+            jax.ShapeDtypeStruct((3, 1, rows), jnp.float32),
             jax.ShapeDtypeStruct((8, 1, rows), jnp.float32),
         ],
-        in_specs=[pl.BlockSpec(memory_space=pltpu.VMEM)] * 5,
-        out_specs=[pl.BlockSpec(memory_space=pltpu.VMEM)] * 2,
+        in_specs=[vmem, vmem, smem, smem],
+        out_specs=[vmem, vmem],
         scratch_shapes=[
+            pltpu.VMEM((3, 3, rows, 1), jnp.float32),
+            pltpu.VMEM((3, rows, 1), jnp.float32),
+            pltpu.VMEM((8, 3, 1, rows), jnp.float32),
+            pltpu.VMEM((8, 1, rows), jnp.float32),
+            pltpu.VMEM((3, rows, rows), jnp.float32),
             pltpu.VMEM((3, rows, width), jnp.bfloat16),
             pltpu.VMEM((8, rows, width), jnp.bfloat16),
             pltpu.SemaphoreType.DMA((4, PIECES)),
@@ -465,7 +509,7 @@
             collective_id=1, has_side_effects=True, vmem_limit_bytes=56 * 1024 * 1024
         ),
         name="pairs",
-    )(unit_rows, lists, gain, klists, kgain)
+    )(unit_rows, labels, neighbours, sharpness)
 
 
 def lookup(table, index):
@@ -480,7 +524,6 @@
     group_index = lax.axis_index("outer")
     owner_index = lax.axis_index("dev")
     clusters = groups * owners
-    group_rows = owners * tokens_here
     cluster_range = jnp.arange(clusters, dtype=jnp.int32)
     sizes = jnp.sum((cluster_of[:, None] == cluster_range[None, :]).astype(jnp.int32), axis=0)
 
@@ -505,33 +548,9 @@
     scaling = lax.rsqrt(jnp.mean(centred * centred, axis=1) + 1e-06) / math.sqrt(feature_width)
     unit_rows = (centred * scaling[:, None]).astype(jnp.bfloat16)
 
-    even = group_index % 2 == 0
-    beside = labels_at(group_index + 1 - 2 * (group_index % 2))
-    across = labels_at(3 - group_index)
-    before = neighbours[:, 2]
-    after = neighbours[:, 3]
-    seen_beside = jnp.where(even, before, after)
-    seen_across = jnp.where(even, after, before)
-    listed = [
-        [own, own, lookup(neighbours[:, 0], own), lookup(neighbours[:, 1], own)],
-        [beside] + [lookup(seen_beside, beside)] * 3,
-        [across] + [lookup(seen_across, across)] * 3,
-    ]
-    lists = jnp.stack([jnp.stack(block) for block in listed])[..., None]
-    gain = jnp.stack([lookup(sharpness, block[0]) for block in listed])[..., None]
-    key_labels = lax.dynamic_slice_in_dim(cluster_of, group_index * group_rows, group_rows)
-    key_shape = (owners, 1, 1, tokens_here)
-    klists = jnp.concatenate(
-        [
-            key_labels.reshape(key_shape),
-            lookup(seen_across, key_labels).reshape(key_shape),
-            lookup(seen_beside, key_labels).reshape(key_shape),
-        ],
-        axis=1,
-    )
-    kgain = lookup(sharpness, key_labels).reshape(owners, 1, tokens_here)
-    acc, cols = paired(unit_rows, lists, gain, klists, kgain)
-    running = returned(cols, jnp.sum(acc, axis=2)[:, None, :])[0]
+    labels = cluster_of.reshape(clusters, 1, tokens_here)
+    rows, cols = paired(unit_rows, labels, neighbours, sharpness)
+    running = returned(cols, rows)[0]
     counts = sizes - 1
     for position in range(neighbours.shape[1]):
         counts = counts + lookup(sizes, neighbours[:, position])

time: 128 us -> 120 us (0.938)
  local copies, waits for them, and re-layouts: 4.67 us -> 1.39 us
  Pallas kernels: 111 us -> 108 us
  other arithmetic: 7.33 us -> 4.84 us
    broadcast_in_dim x3 -> x0, local copies, waits for them, and re-layouts: 2.96 us -> none  [the longest x1 1.46 us: gathered(): lists = jnp.stack([jnp.stack(block) for block in listed])[..., None]]
    pallas_call x1, Pallas kernels: 53.7 us -> 50.9 us  [paired(): pl.pallas_call(pair_kernel, out_shape=[jax.ShapeDtypeStruct((3, 1, rows),...]
where the time goes in v3:
time: 120 us
  Pallas kernels  108 us (90%)
  matrix products  5.66 us (5%)
  other arithmetic  4.84 us (4%)
  local copies, waits for them, and re-layouts  1.39 us (1%)
    pallas_call x1, Pallas kernels, paired(): pl.pallas_call(pair_kernel, out_shape=[jax.ShapeDtypeStruct((3, 1, rows),...  50.9 us
    pallas_call x1, Pallas kernels, returned(): pl.pallas_call(functools.partial(return_kernel, owners), out_shape=jax.Sh...  41.1 us
    pallas_call x1, Pallas kernels, summed(): pl.pallas_call(functools.partial(sum_kernel, owners), out_shape=jax.Shape...  15.6 us
    dot_general x1, matrix products, gathered(): jnp.dot(member.astype(jnp.float32).T, means, precision=lax.Precision.HIGH...  3.3 us

profile of v3, /device:TPU:0, one launch (start us, length us, event | category | flops | bytes accessed | tf_op | source)
XLA Modules:
  0.0 119.5 jit_solution(13956458111869341528)
XLA Ops:
  0.0 0.8 broadcast_subtract_fusion
  0.8 2.4 %fusion.2.part_ref = f32[8,4096]{1,0:T(8,128)} fusion(bf16[192,4096]{1,0:T(8,128)(2,1)} %param.4, s32[192]{0:T(256)S(1)} %get-tuple-element.13), kind=kOutput, calls=%fused_computation.18 | convolution fusion | flops 12584448 | bytes 1704704 | tf_op jit(solution)/shard_map/dot_general | solution.py:538
  3.1 15.6 %mean_sums.1 = f32[8,4096]{1,0:T(8,128)} custom-call(f32[8,4096]{1,0:T(8,128)} %fusion.2.part_ref), custom_call_target="tpu_custom_call" | custom-call | tf_op jit(solution)/shard_map/mean_sums/pallas_call | solution.py:181
  18.7 0.9 convert_reduce_fusion
  19.6 0.1 dynamic-slice_convert_fusion
  19.7 3.3 %multiply_reduce_fusion = (f32[192]{0:T(256)S(1)}, f32[192,4096]{1,0:T(8,128)S(1)}) fusion(f32[8,4096]{1,0:T(8,128)} %mean_sums.1, f32[8]{0:T(128)S(1)} %dynamic-slice_convert_fusion, s32[192]{0:T(256)S(1)} %get-tuple-element.13, bf16[192,4096]{1,0:T(8,128)(2,1)} %param.4), kind=kOutput, calls=%fused_computation.2 | convolution fusion | flops 78677312 | bytes 4851232 | tf_op jit(solution)/shard_map/dot_general | solution.py:541
  23.0 0.0 copy-start
  23.0 0.0 copy-start.1
  23.1 1.5 %multiply_convert_fusion.unit_ref = bf16[192,4096]{1,0:T(8,128)(2,1)} fusion(f32[192,4096]{1,0:T(8,128)S(1)} %get-tuple-element.20, f32[192]{0:T(256)S(1)} %rsqrt_multiply_fusion), kind=kLoop, calls=%fused_computation.1 | loop fusion | flops 1572864 | bytes 4719360 | tf_op jit(solution)/shard_map/convert_element_type | solution.py:549
  24.6 0.0 copy-done
  24.6 0.7 reshape.29.labels_ref
  25.3 0.0 copy-done.1
  25.3 0.7 copy.6.neighbours_ref
  25.9 50.9 %pairs.1 = (f32[3,1,192]{2,1,0:T(1,128)}, f32[8,1,192]{2,1,0:T(1,128)}) custom-call(bf16[192,4096]{1,0:T(8,128)(2,1)} %multiply_convert_fusion.unit_ref, s32[32,1,192]{2,1,0:T(1,128)} %reshape.29.labels_ref, s32[32,4]{1,0:T(8,128)} %copy.6.neighbours_ref, f32[32]{0:T(128)} %sharpness_ref.1), custom_call_target="tpu_custom_call" | custom-call | tf_op jit(solution)/shard_map/pairs/pallas_call | solution.py:487
  76.8 41.1 %return_sums.1 = f32[1,192]{1,0:T(1,128)} custom-call(f32[8,1,192]{2,1,0:T(1,128)} %get-tuple-element.7.cols_ref, f32[3,1,192]{2,1,0:T(1,128)} %get-tuple-element.8.rows_ref), custom_call_target="tpu_custom_call" | custom-call | tf_op jit(solution)/shard_map/return_sums/pallas_call | solution.py:231
  117.9 0.2 select_reduce_fusion.4
  118.2 0.1 select_reduce_fusion
  118.3 1.3 %fusion.5 = f32[192]{0:T(256)} fusion(f32[192]{0:T(256)} %bitcast.10, s32[192]{0:T(256)S(1)} %select_reduce_fusion), kind=kLoop, calls=%fused_computation.23 | loop fusion | flops 384 | bytes 2304 | tf_op jit(solution)/shard_map/log | solution.py:557
  (3 shorter events, 0.0 us)
Async XLA Ops:
  23.0 1.5 %copy-start = (s32[6144]{0:T(1024)S(1)}, s32[6144]{0:T(1024)}, u32[]{:S(2)}) copy-start(s32[6144]{0:T(1024)} %param.5) | copy-start | bytes 73732
  23.0 2.2 %copy-start.1 = (s32[32,4]{0,1:T(4,128)S(1)}, s32[32,4]{0,1:T(4,128)}, u32[]{:S(2)}) copy-start(s32[32,4]{0,1:T(4,128)} %param.6) | copy-start | bytes 1540
